TPU v7x, 128 devices: a whole 4x4x4 slice. The times are simulated.
128 devices in a mesh: rows: 16 (over y, z), trees: 8 (over x, core).
Axes of the slice: x: 4, y: 4, z: 4, core: 2. Of those that a mesh axis runs over, the one named last changes fastest.
Arguments:
- leaf_index: int32 [128, 262144], P(None, ('rows', 'trees')), may hold values from 0 to 31, as said below
- out_of_bag: bfloat16 [128, 262144], P(None, ('rows', 'trees')), may hold values from 0 to 4, as said below
- labels: int32 [262144], P(('rows', 'trees')), may hold values from 0 to 999
Outputs:
- tallies: float32 [128, 32, 1000], P('trees', 'rows')
- tree_error: float32 [128], P('trees')
- forest_error: float32 [], replicated
Inputs may be any that keep to these rules, and one draw needn't show every extreme that they name: `out_of_bag`: 0 exactly where a row was in a tree's sample, else at least 0.25. `leaf_index`: in each tree, the 2048 rows of one device reach every leaf exactly 2048 // 32 times.
All inputs are finite; a program needn't handle non-finite values.
Results may differ from a plain program's by a relative error of at most 0.0003.
Values sent between devices are 32-bit elements; how exact they have to be, the bound alone decides.
No kernel may reach another device: no remote copies, remote signals or barrier semaphores. Data moves between devices by JAX's collectives and lax.ppermute only.
A program may use at most 128 MiB of HBM per device.

v0:
```python
import jax
import jax.numpy as jnp
from jax import lax
from jax.sharding import Mesh
from jax.sharding import PartitionSpec as P

CLASSES = 1000
LEAVES = 32
ROWS = ("rows_0", "rows_1")
TREES = ("trees_0", "trees_1")
ROWS_TREES = ("rows_0", "rows_1", "trees_0", "trees_1")


def in_blocks(shard, dim, peers):
    before, after = (shard.shape[:dim], shard.shape[dim + 1 :])
    return jnp.moveaxis(shard.reshape(*before, peers, -1, *after), dim, 0)


def summed_on_arrival(shard, axis, dim):
    peers = lax.axis_size(axis)
    parts = lax.all_to_all(in_blocks(shard, dim, peers), axis, 0, 0, tiled=True)
    return jnp.sum(parts, axis=0)


def by_axis(shard, axes):
    for axis in axes:
        shard = lax.psum(shard, axis)
    return shard


def count_table(leaves, weights, row_labels, n_rows):
    leaf_block_size = LEAVES // n_rows
    leaf_grid = jnp.arange(LEAVES, dtype=jnp.int32).reshape(n_rows, leaf_block_size)
    class_ids = jnp.arange(CLASSES, dtype=jnp.int32)
    class_onehot = (row_labels[:, None] == class_ids[None, :]).astype(jnp.bfloat16)
    placed = jnp.where(
        leaves[None, :, None, :] == leaf_grid[:, None, :, None],
        weights[None, :, None, :],
        jnp.zeros((), jnp.bfloat16),
    )
    count_grid = jnp.einsum(
        "rtlz,zc->rtlc", placed, class_onehot, preferred_element_type=jnp.float32
    )
    return count_grid.reshape(-1, CLASSES)


def per_device(leaf_index, out_of_bag, labels):
    n_rows = lax.axis_size(ROWS)
    tree_count = lax.axis_size(TREES)
    tree_block = leaf_index.shape[0] // tree_count
    leaf_block_slice = LEAVES // n_rows
    ordered = count_table(leaf_index, out_of_bag, labels, n_rows)
    partial_sum_table = lax.psum_scatter(ordered, ROWS, scatter_dimension=0, tiled=True)
    owned_part = summed_on_arrival(partial_sum_table, TREES, 0)
    tallies = owned_part.reshape(tree_block, leaf_block_slice, CLASSES)
    leaf_total = jnp.sum(tallies, axis=2)
    leaf_top = jnp.max(tallies, axis=2)
    local_wrong = jnp.sum(leaf_total - leaf_top, axis=1)
    local_seen = jnp.sum(leaf_total, axis=1)
    wrong_sum, seen_sum = (by_axis(local_wrong, ROWS), by_axis(local_seen, ROWS))
    tree_error = wrong_sum / seen_sum
    all_wrong, all_seen = (
        by_axis(jnp.sum(local_wrong), ROWS_TREES),
        by_axis(jnp.sum(local_seen), ROWS_TREES),
    )
    forest_error = all_wrong / all_seen
    return (tallies, tree_error, forest_error)


def solution(mesh):
    split = Mesh(mesh.devices.reshape(4, 4, 4, 2), ("rows_0", "rows_1", "trees_0", "trees_1"))
    placed = (P(None, ROWS_TREES), P(None, ROWS_TREES), P(ROWS_TREES))
    return jax.shard_map(
        per_device,
        mesh=split,
        in_specs=placed,
        out_specs=(P(TREES, ROWS, None), P(TREES), P()),
        check_vma=False,
    )
```

profile of v0, /device:TPU:1, one launch (start us, length us, event | category | flops | bytes accessed | tf_op | source)
XLA Modules:
  0.0 254.7 jit_solution(17443909807189443048)
XLA Ops:
  7.2 0.0 reduce-scatter.2.cloned.1.call-start
  7.2 21.7 %fusion = f32[16,128,2,1000]{1,3,2,0:T(8,128)} fusion(s32[16,2]{1,0:T(8,128)S(1)} %multiply_add_fusion, s32[128,2048]{1,0:T(8,128)} %param.3, bf16[128,2048]{1,0:T(8,128)(2,1)} %param.4, s32[2048]{0:T(1024)} %param.5), kind=kOutput, calls=%fused_computation.1 | convolution fusion | flops 16796041216 | bytes 17965184 | tf_op jit(solution)/shard_map/rtlz,zc->rtlc/dot_general | solution.py:41
  29.0 25.1 %copy.6 = f32[16,128,2,1000]{3,2,1,0:T(2,128)} copy(f32[16,128,2,1000]{1,3,2,0:T(8,128)} %fusion) | data formatting | bytes 32768000 | tf_op jit(solution)/shard_map/rtlz,zc->rtlc/dot_general | solution.py:41
  54.0 20.8 %reshape.34 = f32[4096,1000]{1,0:T(8,128)} reshape(f32[16,128,2,1000]{3,2,1,0:T(2,128)} %copy.6) | data formatting | bytes 32768000 | tf_op jit(solution)/shard_map/reshape | solution.py:44
  74.8 0.0 reduce-scatter.2.cloned.1.call-update
  74.8 114.0 %reduce-scatter.2.cloned.1.call-done = f32[256,1000]{1,0:T(8,128)} async-done(((f32[4096,1000]{1,0:T(8,128)}), f32[256,1000]{1,0:T(8,128)}) %reduce-scatter.2.cloned.1.call-update) | async-done | bytes 1024016 | tf_op jit(solution)/shard_map/reduce_scatter | solution.py:53
  188.9 20.1 %all_to_all.5 = f32[8,32,1000]{2,1,0:T(8,128)S(1)} all-to-all(f32[8,32,1000]{2,1,0:T(8,128)} %bitcast.6), channel_id=1, replica_groups=mesh['rows_0'=4,'rows_1'=4,'trees_0'=4,'trees_1'=2] {'trees_0','trees_1'}, dimensions={0} | all-to-all | bytes 2048000 | tf_op jit(solution)/shard_map/all_to_all | solution.py:21
  209.0 0.9 fusion.9
  209.9 0.7 reshape.36
  210.6 0.1 reduce_max.11
  210.7 0.1 reduce_max.12
  210.8 0.6 subtract_reduce_fusion.1
  211.4 0.1 reduce_sum.58
  211.5 0.1 fusion.10
  211.6 8.7 %all-reduce.2 = (f32[16]{0:T(128)S(1)}, f32[16]{0:T(128)S(1)}, f32[]{:T(128)}, f32[]{:T(128)}) all-reduce(f32[16]{0:T(128)S(1)} %get-tuple-element.7, f32[16]{0:T(128)S(1)} %get-tuple-element.6, f32[]{:T(128)} %subtract_reduce_fusion.1, f32[]{:T(128)} %get-tuple-element.3), channel_id=1, replica_groups=mesh['rows_0'=4,'rows_1'=4,'trees_0'=4,'trees_1'=2] {'rows_0'}, use_global_device_ids=true, to_apply=%region_5.6 | all-reduce | flops 34 | bytes 272 | tf_op jit(solution)/shard_map/psum | solution.py:27
  220.3 7.4 %all-reduce.1 = (f32[16]{0:T(128)S(1)}, f32[16]{0:T(128)S(1)}, f32[]{:T(128)}, f32[]{:T(128)}) all-reduce(f32[16]{0:T(128)S(1)} %get-tuple-element.14, f32[16]{0:T(128)S(1)} %get-tuple-element.15, f32[]{:T(128)} %get-tuple-element.16, f32[]{:T(128)} %get-tuple-element.17), channel_id=1, replica_groups=mesh['rows_0'=4,'rows_1'=4,'trees_0'=4,'trees_1'=2] {'rows_1'}, use_global_device_ids=true, to_apply=%region_6.7 | all-reduce | flops 34 | bytes 272 | tf_op jit(solution)/shard_map/psum | solution.py:27
  227.7 0.5 div.6
  228.2 7.6 %all-reduce = (f32[]{:T(128)}, f32[]{:T(128)}) all-reduce(f32[]{:T(128)} %get-tuple-element.12, f32[]{:T(128)} %get-tuple-element.13), channel_id=1, replica_groups=mesh['rows_0'=4,'rows_1'=4,'trees_0'=4,'trees_1'=2] {'trees_0'}, use_global_device_ids=true, to_apply=%region_13.14 | all-reduce | flops 2 | bytes 16 | tf_op jit(solution)/shard_map/psum | solution.py:27
  235.8 9.7 %all-reduce.3 = (f32[]{:T(128)}, f32[]{:T(128)}) all-reduce(f32[]{:T(128)} %get-tuple-element.8, f32[]{:T(128)} %get-tuple-element.9), channel_id=1, replica_groups=mesh['rows_0'=4,'rows_1'=4,'trees_0'=4,'trees_1'=2] {'trees_1'}, use_global_device_ids=true, to_apply=%region_14.15 | all-reduce | flops 2 | bytes 16 | tf_op jit(solution)/shard_map/psum | solution.py:27
  (1 shorter events, 0.0 us)
Async XLA Ops:
  7.2 181.7 %reduce-scatter.2.cloned.1.call-start = ((), (), s32[]{:S(2)}) async-start(), calls=%async_computation.2 | async-start | bytes 17825792 | tf_op jit(solution)/shard_map/reduce_scatter | solution.py:53
Sparse Core Ops, SparseCore 0:
  74.9 113.8 reduce-scatter.1
where the time goes:
time: 256 us; the launch traced here: 255 us
  waiting for transfers between devices  114 us (45%)
  blocking collectives  53.4 us (21%)
  local copies, waits for them, and re-layouts  46.7 us (18%)
  matrix products  21.7 us (8%)
  between operations  16.4 us (6%)
    reduce_scatter x1, waiting for transfers between devices, per_device(): lax.psum_scatter(ordered, ROWS, scatter_dimension=0, tiled=True)  114 us
    psum x4, blocking collectives, by_axis(): shard = lax.psum(shard, axis)  33.3 us
    dot_general x1, local copies, waits for them, and re-layouts, count_table(): jnp.einsum('rtlz,zc->rtlc', placed, class_onehot, preferred_element_type=...  25.1 us
    dot_general x1, matrix products, count_table(): jnp.einsum('rtlz,zc->rtlc', placed, class_onehot, preferred_element_type=...  21.7 us
    reshape x1, local copies, waits for them, and re-layouts, count_table(): return count_grid.reshape(-1, CLASSES)  20.8 us
    all_to_all x1, blocking collectives, summed_on_arrival(): parts = lax.all_to_all(in_blocks(shard, dim, peers), axis, 0, 0, tiled=True)  20.1 us
  transfers between devices with their start and end apart: 1, of which 1 were waited for; matrix products, arithmetic and copies ran while one was open for 0% of the time, Pallas kernels for 0%

commit v1 on v0

--- a/solution.py
+++ b/solution.py
@@ -24,7 +24,7 @@
 
 def by_axis(shard, axes):
     for axis in axes:
-        shard = lax.psum(shard, axis)
+        shard = jnp.sum(lax.all_gather(shard, axis), axis=0)
     return shard
 
 

time: 256 us -> 271 us (1.059)
  blocking collectives: 53.4 us -> 30.6 us
  local copies, waits for them, and re-layouts: 46.7 us -> 61.5 us
  waiting for transfers between devices: 114 us -> 125 us
  starting transfers between devices: 0.04 us -> 5.2 us
  other arithmetic: 2.27 us -> 7.24 us
    psum x4 -> x0, blocking collectives: 33.3 us -> none  [by_axis(): shard = lax.psum(shard, axis)]
    unnamed x0 -> x4, blocking collectives: none -> 30.6 us
    all_to_all x1 -> x0, blocking collectives: 20.1 us -> none  [summed_on_arrival(): parts = lax.all_to_all(in_blocks(shard, dim, peers), axis, 0, 0, tiled=True)]
    unnamed x0 -> x36, local copies, waits for them, and re-layouts: none -> 14.5 us
    all_to_all x0 -> x1, waiting for transfers between devices: none -> 11.2 us  [summed_on_arrival(): parts = lax.all_to_all(in_blocks(shard, dim, peers), axis, 0, 0, tiled=True)]
    all_to_all x0 -> x1, starting transfers between devices: none -> 5.16 us  [summed_on_arrival(): parts = lax.all_to_all(in_blocks(shard, dim, peers), axis, 0, 0, tiled=True)]
    reduce_sum x0 -> x12, other arithmetic: none -> 4.89 us  [by_axis(): shard = jnp.sum(lax.all_gather(shard, axis), axis=0)]
  transfers between devices with their start and end apart: 1 -> 2, of which waited for: 1 -> 2; matrix products, arithmetic and copies ran while one was open for 0% -> 1% of each run, Pallas kernels for 0% -> 0%
where the time goes in v1:
time: 271 us; the launch traced here: 269 us
  waiting for transfers between devices  125 us (46%)
  local copies, waits for them, and re-layouts  61.5 us (23%)
  blocking collectives  30.6 us (11%)
  matrix products  21.7 us (8%)
  between operations  17.9 us (7%)
  other arithmetic  7.24 us (3%)
  starting transfers between devices  5.2 us (2%)
    reduce_scatter x1, waiting for transfers between devices, per_device(): lax.psum_scatter(ordered, ROWS, scatter_dimension=0, tiled=True)  114 us
    unnamed x4, blocking collectives  30.6 us
    dot_general x1, local copies, waits for them, and re-layouts, count_table(): jnp.einsum('rtlz,zc->rtlc', placed, class_onehot, preferred_element_type=...  25.1 us
    dot_general x1, matrix products, count_table(): jnp.einsum('rtlz,zc->rtlc', placed, class_onehot, preferred_element_type=...  21.7 us
    reshape x1, local copies, waits for them, and re-layouts, count_table(): return count_grid.reshape(-1, CLASSES)  20.8 us
    unnamed x36, local copies, waits for them, and re-layouts  14.5 us
    all_to_all x1, waiting for transfers between devices, summed_on_arrival(): parts = lax.all_to_all(in_blocks(shard, dim, peers), axis, 0, 0, tiled=True)  11.2 us
  transfers between devices with their start and end apart: 2, of which 2 were waited for; matrix products, arithmetic and copies ran while one was open for 1% of the time, Pallas kernels for 0%

profile of v1, /device:TPU:1, one launch (start us, length us, event | category | flops | bytes accessed | tf_op | source)
XLA Modules:
  0.0 269.4 jit_solution(9729830474851254904)
XLA Ops:
  7.2 0.0 reduce-scatter.2.cloned.1.call-start
  7.2 21.7 %fusion = f32[16,128,2,1000]{1,3,2,0:T(8,128)} fusion(s32[16,2]{1,0:T(8,128)S(1)} %multiply_add_fusion, s32[128,2048]{1,0:T(8,128)} %param.3, bf16[128,2048]{1,0:T(8,128)(2,1)} %param.4, s32[2048]{0:T(1024)} %param.5), kind=kOutput, calls=%fused_computation.1 | convolution fusion | flops 16796041216 | bytes 17965184 | tf_op jit(solution)/shard_map/rtlz,zc->rtlc/dot_general | solution.py:41
  29.0 25.1 %copy.6 = f32[16,128,2,1000]{3,2,1,0:T(2,128)} copy(f32[16,128,2,1000]{1,3,2,0:T(8,128)} %fusion) | data formatting | bytes 32768000 | tf_op jit(solution)/shard_map/rtlz,zc->rtlc/dot_general | solution.py:41
  54.0 20.8 %reshape.34 = f32[4096,1000]{1,0:T(8,128)} reshape(f32[16,128,2,1000]{3,2,1,0:T(2,128)} %copy.6) | data formatting | bytes 32768000 | tf_op jit(solution)/shard_map/reshape | solution.py:44
  74.8 0.0 copy-start.3
  74.8 0.0 copy-start.2
  74.8 0.0 copy-start.1
  74.8 0.0 copy-start
  74.8 0.0 reduce-scatter.2.cloned.1.call-update
  74.8 114.0 %reduce-scatter.2.cloned.1.call-done = f32[256,1000]{1,0:T(8,128)} async-done(((f32[4096,1000]{1,0:T(8,128)}), f32[256,1000]{1,0:T(8,128)}) %reduce-scatter.2.cloned.1.call-update) | async-done | bytes 1024016 | tf_op jit(solution)/shard_map/reduce_scatter | solution.py:53
  188.9 5.2 %all-to-all-start = ((f32[8,32,1000]{2,1,0:T(8,128)}), f32[8,32,1000]{2,1,0:T(8,128)S(1)}, u32[]{:S(2)}, u32[]{:S(2)}) async-start(f32[8,32,1000]{2,1,0:T(8,128)} %bitcast.20), calls=%async_computation.1 | async-start | bytes 2097152 | tf_op jit(solution)/shard_map/all_to_all | solution.py:21
  194.0 0.0 copy-done.3
  194.0 0.6 dynamic-slice
  194.6 0.0 copy-done.2
  194.6 0.7 dynamic-slice.1
  196.6 0.0 copy-done.1
  196.6 0.6 dynamic-slice.6
  197.2 0.0 copy-done
  197.2 0.6 dynamic-slice.7
  197.8 11.2 %all-to-all-done = f32[8,32,1000]{2,1,0:T(8,128)S(1)} async-done(((f32[8,32,1000]{2,1,0:T(8,128)}), f32[8,32,1000]{2,1,0:T(8,128)S(1)}, u32[]{:S(2)}, u32[]{:S(2)}) %all-to-all-start) | async-done | bytes 1024032 | tf_op jit(solution)/shard_map/all_to_all | solution.py:21
  209.0 0.9 fusion.9
  209.9 0.1 reduce_max.11
  210.0 0.1 reduce_max.12
  210.1 0.1 reduce_sum.166
  210.2 0.7 subtract_reduce_fusion.1
  210.9 0.7 reshape.36
  211.6 0.1 fusion.10
  211.7 0.2 dynamic-update-slice.2
  212.0 0.2 dynamic-update-slice
  212.2 1.4 dynamic-update-slice.4
  213.6 1.4 dynamic-update-slice.8
  215.0 8.0 %all-reduce.14 = (f32[64]{0:T(128)S(1)}, f32[64]{0:T(128)S(1)}, f32[4]{0:T(128)S(1)}, f32[4]{0:T(128)S(1)}) all-reduce(f32[64]{0:T(128)S(1)} %dynamic-update-slice, f32[64]{0:T(128)S(1)} %dynamic-update-slice.2, f32[4]{0:T(128)S(1)} %dynamic-update-slice.4, ...), channel_id=2, replica_groups=mesh['rows_0'=4,'rows_1'=4,'trees_0'=4,'trees_1'=2] {'rows_0'}, use_global_device_ids=true, to_apply=%add | all-reduce | flops 136 | bytes 1088
  223.1 0.1 reshape.39
  223.1 0.1 reshape.37
  223.3 0.2 dynamic-update-slice.3
  223.5 0.2 dynamic-update-slice.1
  223.7 0.6 reduce_sum.174
  224.3 0.6 reduce_sum.179
  224.9 1.4 dynamic-update-slice.5
  226.4 1.4 dynamic-update-slice.9
  227.8 6.7 %all-reduce.13 = (f32[64]{0:T(128)S(1)}, f32[64]{0:T(128)S(1)}, f32[4]{0:T(128)S(1)}, f32[4]{0:T(128)S(1)}) all-reduce(f32[64]{0:T(128)S(1)} %dynamic-update-slice.1, f32[64]{0:T(128)S(1)} %dynamic-update-slice.3, f32[4]{0:T(128)S(1)} %dynamic-update-slice.5, ...), channel_id=3, replica_groups=mesh['rows_0'=4,'rows_1'=4,'trees_0'=4,'trees_1'=2] {'rows_1'}, use_global_device_ids=true, to_apply=%add.1 | all-reduce | flops 136 | bytes 1088
  234.5 0.6 reduce_sum.180
  235.1 0.6 reduce_sum.175
  235.7 1.3 dynamic-update-slice.10
  237.0 1.3 dynamic-update-slice.6
  238.3 0.1 reshape.38
  238.4 6.9 %all-reduce.12 = (f32[4]{0:T(128)S(1)}, f32[4]{0:T(128)S(1)}) all-reduce(f32[4]{0:T(128)S(1)} %dynamic-update-slice.6, f32[4]{0:T(128)S(1)} %dynamic-update-slice.10), channel_id=1, replica_groups=mesh['rows_0'=4,'rows_1'=4,'trees_0'=4,'trees_1'=2] {'trees_0'}, use_global_device_ids=true, to_apply=%add.6 | all-reduce | flops 8 | bytes 64
  245.3 0.6 reduce_sum.181
  245.9 0.6 reduce_sum.176
  246.5 1.4 dynamic-update-slice.11
  247.9 1.4 dynamic-update-slice.7
  249.2 0.1 reshape.40
  249.3 9.0 %all-reduce.15 = (f32[2]{0:T(128)S(1)}, f32[2]{0:T(128)S(1)}) all-reduce(f32[2]{0:T(128)S(1)} %dynamic-update-slice.7, f32[2]{0:T(128)S(1)} %dynamic-update-slice.11), channel_id=1, replica_groups=mesh['rows_0'=4,'rows_1'=4,'trees_0'=4,'trees_1'=2] {'trees_1'}, use_global_device_ids=true, to_apply=%add.7 | all-reduce | flops 4 | bytes 32
  258.4 0.6 reduce_sum.177
  259.0 0.6 reduce_sum.182
  260.9 0.5 div.6
  (17 shorter events, 0.1 us)
Async XLA Ops:
  7.2 181.7 %reduce-scatter.2.cloned.1.call-start = ((), (), s32[]{:S(2)}) async-start(), calls=%async_computation.2 | async-start | bytes 17825792 | tf_op jit(solution)/shard_map/reduce_scatter | solution.py:53
  74.8 119.2 %copy-start.3 = (u32[128]{0:T(128)S(1)}, u32[128]{0:T(128)}, u32[]{:S(2)}) copy-start(u32[128]{0:T(128)} %constant.12) | copy-start | bytes 1540
  74.8 119.8 %copy-start.2 = (u32[128]{0:T(128)S(1)}, u32[128]{0:T(128)}, u32[]{:S(2)}) copy-start(u32[128]{0:T(128)} %constant.17) | copy-start | bytes 1540
  74.8 121.8 %copy-start.1 = (u32[128]{0:T(128)S(1)}, u32[128]{0:T(128)}, u32[]{:S(2)}) copy-start(u32[128]{0:T(128)} %constant.42) | copy-start | bytes 1540
  74.8 122.4 %copy-start = (u32[128]{0:T(128)S(1)}, u32[128]{0:T(128)}, u32[]{:S(2)}) copy-start(u32[128]{0:T(128)} %constant.47) | copy-start | bytes 1540
  188.9 20.1 %all-to-all-start = ((f32[8,32,1000]{2,1,0:T(8,128)}), f32[8,32,1000]{2,1,0:T(8,128)S(1)}, u32[]{:S(2)}, u32[]{:S(2)}) async-start(f32[8,32,1000]{2,1,0:T(8,128)} %bitcast.20), calls=%async_computation.1 | async-start | bytes 2097152 | tf_op jit(solution)/shard_map/all_to_all | solution.py:21
Sparse Core Ops, SparseCore 0:
  75.0 113.8 reduce-scatter.1
